TPU v7x, 32 devices: a whole 2x2x4 slice. The times are simulated.
32 devices in a mesh: heads: 4 (over y, core), tokens: 4 (over z), cols: 2 (over x).
Axes of the slice: x: 2, y: 2, z: 4, core: 2. Of those that a mesh axis runs over, the one named last changes fastest.
Arguments:
- query_in: bfloat16 [2048, 8192], P('tokens', ('heads', 'cols')), may hold values from -24 to 24
- key_in: bfloat16 [2048, 8192], P('tokens', ('heads', 'cols')), may hold values from -24 to 24
- value_in: bfloat16 [2048, 8192], P('tokens', ('heads', 'cols')), may hold values from -6 to 6
- out_grads: bfloat16 [2048, 8192], P('tokens', ('heads', 'cols')), may hold values from -6 to 6
- doc_starts: int32 [6], replicated, may hold values from 0 to 2047, as said below
Outputs:
- input_factor: float32 [8192, 8192], P('heads', ('tokens', 'cols'))
- grad_factor: float32 [8192, 8192], P('heads', ('tokens', 'cols'))
Inputs may be any that keep to these rules, and one draw needn't show every extreme that they name: Strictly increasing with the first entry 0; document d runs from doc_starts[d] to the next start (the last one to 2048) - 1. One document holds (4 // 2 + 1) * 512 tokens.
All inputs are finite; a program needn't handle non-finite values.
Results may differ from a plain program's by a relative error of at most 0.0041.
Values may be sent and summed in bfloat16 or wider, within the bound.
A program may use at most 128 MiB of HBM per device.

v0:
```python
import math
import jax
import jax.numpy as jnp
from jax import lax
from jax.sharding import PartitionSpec as P

HEAD_DIM = 128
MASK_FLOOR = -1e30


def spread(value, axis, source):
    kept = jnp.where(lax.axis_index(axis) == source, value, 0).astype(value.dtype)
    return lax.psum(kept, axis)


def document_ids(positions, doc_starts):
    return jnp.sum((positions[:, None] >= doc_starts[None, :]).astype(jnp.int32), axis=1) - 1


def pair_scores(query_rows, key_rows, query_pos, key_pos, doc_starts):
    head_count = query_rows.shape[1] // HEAD_DIM
    query_heads = query_rows.reshape(query_rows.shape[0], head_count, HEAD_DIM)
    key_heads = key_rows.reshape(key_rows.shape[0], head_count, HEAD_DIM)
    scores = jnp.einsum(
        "qhd,khd->hqk", query_heads, key_heads, preferred_element_type=jnp.float32
    ) * (1.0 / math.sqrt(HEAD_DIM))
    query_docs = document_ids(query_pos, doc_starts)
    key_docs = document_ids(key_pos, doc_starts)
    allowed = query_docs[:, None] == key_docs[None, :]
    return (scores, allowed[None, :, :])


def on_device(query_in, key_in, value_in, out_grads, doc_starts):
    tok_dev, row_width = query_in.shape
    head_count = row_width // HEAD_DIM
    first_pos = lax.axis_index("tokens") * tok_dev
    query_pos = first_pos + jnp.arange(tok_dev, dtype=jnp.int32)
    keys_all, values_all = (
        lax.all_gather(key_in, "tokens", axis=0, tiled=True),
        lax.all_gather(value_in, "tokens", axis=0, tiled=True),
    )
    all_tokens = keys_all.shape[0]
    key_span = min(512, all_tokens)
    block_ids = jnp.arange(all_tokens // key_span, dtype=jnp.int32)

    def block_scores(block_id):
        key_begin = block_id * key_span
        key_rows = lax.dynamic_slice_in_dim(keys_all, key_begin, key_span, 0)
        key_pos = key_begin + jnp.arange(key_span, dtype=jnp.int32)
        scores, allowed = pair_scores(query_in, key_rows, query_pos, key_pos, doc_starts)
        return (key_begin, scores, allowed)

    def gated(block_id, update, running):
        key_begin = block_id * key_span
        return update(running)

    def stats_step(running, block_id):

        def update(state):
            row_peak, row_mass = state
            key_begin, scores, allowed = block_scores(block_id)
            masked = jnp.where(allowed, scores, MASK_FLOOR)
            new_peak = jnp.maximum(row_peak, jnp.max(masked, axis=2))
            new_mass = row_mass * jnp.exp(row_peak - new_peak) + jnp.sum(
                jnp.where(allowed, jnp.exp(masked - new_peak[:, :, None]), 0.0), axis=2
            )
            return (new_peak, new_mass)

        return (gated(block_id, update, running), None)

    initial = (
        jnp.full((head_count, tok_dev), MASK_FLOOR, jnp.float32),
        jnp.zeros((head_count, tok_dev), jnp.float32),
    )
    (row_peak, row_mass), _ = lax.scan(stats_step, initial, block_ids)
    log_total = row_peak + jnp.log(row_mass)

    def value_step(running, block_id):

        def update(state):
            weighted, partials = state
            key_begin, scores, allowed = block_scores(block_id)
            weights = jnp.where(allowed, jnp.exp(scores - log_total[:, :, None]), 0.0).astype(
                jnp.bfloat16
            )
            value_rows = lax.dynamic_slice_in_dim(values_all, key_begin, key_span, 0).reshape(
                key_span, head_count, HEAD_DIM
            )
            weighted = weighted + jnp.einsum(
                "hqk,khd->qhd", weights, value_rows, preferred_element_type=jnp.float32
            )
            return (weighted, partials)

        return (gated(block_id, update, running), None)

    partial_rows = 8
    value_init = (
        jnp.zeros((tok_dev, head_count, HEAD_DIM), jnp.float32),
        jnp.zeros((partial_rows, row_width), jnp.float32),
    )
    (weighted, partials), _ = lax.scan(value_step, value_init, block_ids)
    attended = weighted.reshape(tok_dev, row_width).astype(jnp.bfloat16)
    stats_all = lax.all_gather(log_total.T, "tokens", axis=0, tiled=True)
    query_rows = lax.all_gather(query_in, "tokens", axis=0, tiled=True)
    grad_rows = lax.all_gather(out_grads, "tokens", axis=0, tiled=True)
    piece_rows = query_rows.shape[0]
    piece_pos = jnp.arange(piece_rows, dtype=jnp.int32)

    def update(grad_sum):
        scores, allowed = pair_scores(query_rows, key_in, piece_pos, query_pos, doc_starts)
        weights = jnp.where(allowed, jnp.exp(scores - stats_all.T[:, :, None]), 0.0).astype(
            jnp.bfloat16
        )
        piece_grads = grad_rows.reshape(piece_rows, head_count, HEAD_DIM)
        return jnp.einsum("hqk,qhd->khd", weights, piece_grads, preferred_element_type=jnp.float32)

    summed = update(jnp.zeros((tok_dev, head_count, HEAD_DIM), jnp.float32))
    value_grads = summed.reshape(tok_dev, row_width).astype(jnp.bfloat16)
    token_shards = lax.axis_size("tokens")
    col_shards = lax.axis_size("cols")
    rows_attended, rows_grads = (
        lax.all_gather(attended[None], ("tokens", "cols"), axis=0, tiled=True),
        lax.all_gather(value_grads[None], ("tokens", "cols"), axis=0, tiled=True),
    )
    rows_attended = rows_attended.reshape(token_shards, col_shards, tok_dev, row_width)
    rows_grads = rows_grads.reshape(token_shards, col_shards, tok_dev, row_width)
    own_attended = lax.dynamic_index_in_dim(
        rows_attended, lax.axis_index("cols"), 1, keepdims=False
    )
    own_grads = lax.dynamic_index_in_dim(rows_grads, lax.axis_index("cols"), 1, keepdims=False)
    cols_attended, cols_grads = (
        spread(own_attended, "heads", lax.axis_index("tokens")),
        spread(own_grads, "heads", lax.axis_index("tokens")),
    )
    input_factor = jnp.einsum(
        "acnf,ang->cfg", rows_attended, cols_attended, preferred_element_type=jnp.float32
    )
    grad_factor = jnp.einsum(
        "acnf,ang->cfg", rows_grads, cols_grads, preferred_element_type=jnp.float32
    )
    input_factor = input_factor.reshape(col_shards * row_width, row_width) / all_tokens
    grad_factor = grad_factor.reshape(col_shards * row_width, row_width) / all_tokens
    return (input_factor, grad_factor)


def solution(mesh):
    in_specs = (
        P("tokens", ("heads", "cols")),
        P("tokens", ("heads", "cols")),
        P("tokens", ("heads", "cols")),
        P("tokens", ("heads", "cols")),
        P(),
    )
    out_specs = (P("heads", ("tokens", "cols")), P("heads", ("tokens", "cols")))
    return jax.shard_map(
        on_device, mesh=mesh, in_specs=in_specs, out_specs=out_specs, check_vma=False
    )
```

profile of v0, /device:TPU:0, one launch (start us, length us, event | category | flops | bytes accessed | tf_op | source)
XLA Modules:
  0.0 775.8 jit_solution(3249628128545039161)
XLA Ops:
  7.2 2.4 copy.58
  9.7 2.3 copy.57
  12.0 0.7 all-gather.15.cloned.1.call-update
  12.8 2.3 copy.62
  15.1 78.1 %all-gather.9.cloned.1.call-done = bf16[2048,1024]{0,1:T(8,128)(2,1)} async-done(((bf16[512,1024]{0,1:T(8,128)(2,1)}), bf16[2048,1024]{0,1:T(8,128)(2,1)}) %all-gather.9.cloned.1.call-update) | async-done | bytes 4194320 | tf_op jit(solution)/shard_map/all_gather | solution.py:39
  93.2 27.0 %while.30 = (s32[]{:T(128)}, f32[8,512]{1,0:T(8,128)S(1)}, f32[8,512]{1,0:T(8,128)S(1)}, s32[6]{0:T(128)S(1)}, s32[4]{0:T(128)S(1)}, /*index=5*/bf16[2048,1024]{...) while((s32[]{:T(128)}, f32[8,512]{1,0:T(8,128)S(1)}, ...), condition=%wide.region_5.6_spmd.clone, body=%wide.region_0.5_spmd.clone.sunk | while | flops 553950208 | bytes 21995748 | solution.py:75
  93.2 0.6 dynamic_slice.60
  94.6 0.2 broadcast_compare_fusion.5
  94.8 1.3 constant_dynamic-slice_fusion.5
  96.1 1.7 fusion.59
  97.9 2.0 select_reduce_fusion.2
  100.0 0.6 dynamic_slice.60
  101.3 0.2 broadcast_compare_fusion.5
  101.5 1.4 constant_dynamic-slice_fusion.5
  102.9 1.7 fusion.59
  104.7 2.0 select_reduce_fusion.2
  106.8 0.6 dynamic_slice.60
  108.2 0.2 broadcast_compare_fusion.5
  108.4 1.3 constant_dynamic-slice_fusion.5
  109.7 1.7 fusion.59
  111.4 2.0 select_reduce_fusion.2
  113.5 0.6 dynamic_slice.60
  114.9 0.2 broadcast_compare_fusion.5
  115.1 1.3 constant_dynamic-slice_fusion.5
  116.4 1.7 fusion.59
  118.2 2.0 select_reduce_fusion.2
  120.3 54.3 %all-gather.7.cloned.1.call-done = bf16[2048,1024]{0,1:T(8,128)(2,1)} async-done(((bf16[512,1024]{0,1:T(8,128)(2,1)}), bf16[2048,1024]{0,1:T(8,128)(2,1)}) %all-gather.7.cloned.1.call-update) | async-done | bytes 4194320 | tf_op jit(solution)/shard_map/all_gather | solution.py:40
  174.6 34.2 %while.31 = (s32[]{:T(128)}, f32[512,8,128]{0,2,1:T(8,128)}, s32[4]{0:T(128)S(1)}, bf16[2048,1024]{0,1:T(8,128)(2,1)}, s32[6]{0:T(128)S(1)}, /*index=5*/bf16[204...) while((s32[]{:T(128)}, f32[512,8,128]{0,2,1:T(8,128)}, ...), condition=%wide.region_9.10_spmd.clone, body=%wide.region_6.9_spmd.clone.sunk | while | flops 1083460608 | bytes 12099821 | solution.py:101
  174.6 0.6 dynamic_slice.62
  176.0 0.2 broadcast_compare_fusion.6
  176.2 1.7 constant_dynamic-slice_fusion.6
  177.9 4.0 bitcast_add_fusion.2
  181.9 0.6 dynamic_slice.62
  183.3 0.2 broadcast_compare_fusion.6
  183.5 1.9 constant_dynamic-slice_fusion.6
  185.4 5.6 bitcast_add_fusion.2
  191.0 0.6 dynamic_slice.62
  192.4 0.2 broadcast_compare_fusion.6
  192.6 1.7 constant_dynamic-slice_fusion.6
  194.3 5.6 bitcast_add_fusion.2
  199.9 0.6 dynamic_slice.62
  201.3 0.2 broadcast_compare_fusion.6
  201.5 1.7 constant_dynamic-slice_fusion.6
  203.2 5.6 bitcast_add_fusion.2
  208.8 1.8 convert_element_type.76
  210.7 1.3 copy.73
  212.1 0.1 convert_reduce_fusion.4
  212.3 0.8 broadcast_compare_fusion.2
  213.0 42.4 %all-gather.15.cloned.1.call-done = bf16[2048,1024]{1,0:T(8,128)(2,1)} async-done(((bf16[512,1024]{1,0:T(8,128)(2,1)}), bf16[2048,1024]{1,0:T(8,128)(2,1)}) %all-gather.15.cloned.1.call-update) | async-done | bytes 4194320 | tf_op jit(solution)/shard_map/all_gather | solution.py:105
  255.5 6.4 copy.65
  261.9 15.2 %all_gather.25 = f32[2048,8]{0,1:T(8,128)S(1)} all-gather(f32[512,8]{0,1:T(8,128)S(1)} %bitcast.132), channel_id=1, replica_groups=mesh['heads'=4,'tokens'=4,'cols'=2] {'tokens'}, dimensions={0}, use_global_device_ids=true | all-gather | bytes 81920 | tf_op jit(solution)/shard_map/all_gather | solution.py:103
  277.1 59.8 %all-gather.13.cloned.1.call-done = bf16[2048,1024]{0,1:T(8,128)(2,1)} async-done(((bf16[512,1024]{0,1:T(8,128)(2,1)}), bf16[2048,1024]{0,1:T(8,128)(2,1)}) %all-gather.13.cloned.1.call-update) | async-done | bytes 4194320 | tf_op jit(solution)/shard_map/all_gather | solution.py:104
  336.9 14.4 %fusion.29 = bf16[8,512,128]{1,2,0:T(8,128)(2,1)S(1)} fusion(bf16[2048,8,128]{0,2,1:T(8,128)(2,1)} %bitcast.130, bf16[2048,8,128]{0,2,1:T(8,128)(2,1)} %bitcast.134, f32[8,2048]{1,0:T(8,128)S(1)} %bitcast.133, pred[2048,512]{1,0:T(8,128)(4,1)S(1)} %broadcast_compare_fusion.2, bf16[512,1024]{1,0:T(8,128)(2,1)S(1)} %copy-done.2), kind=kOutput, calls=%fused_computation.50 | convolution fusion | flops 4329046016 | bytes 11599872 | tf_op jit(solution)/shard_map/hqk,qhd->khd/dot_general | solution.py:115
  351.3 1.3 copy.66
  352.7 0.3 all-reduce.3.cloned.1.call-start
  353.0 109.4 %all-gather.11.cloned.1.call-done = bf16[8,512,1024]{2,1,0:T(8,128)(2,1)} async-done(((bf16[1,512,1024]{2,1,0:T(8,128)(2,1)}), bf16[8,512,1024]{2,1,0:T(8,128)(2,1)}) %all-gather.11.cloned.1.call-update) | async-done | bytes 8388624 | tf_op jit(solution)/shard_map/all_gather | solution.py:122
  462.4 4.5 fusion.27
  466.9 120.8 %all-gather.17.cloned.1.call-done = bf16[8,512,1024]{2,1,0:T(8,128)(2,1)} async-done(((bf16[1,512,1024]{2,1,0:T(8,128)(2,1)}), bf16[8,512,1024]{2,1,0:T(8,128)(2,1)}) %all-gather.17.cloned.1.call-update) | async-done | bytes 8388624 | tf_op jit(solution)/shard_map/all_gather | solution.py:123
  587.6 4.4 fusion.26
  592.1 11.5 %copy.60 = bf16[2,1024,4,512]{3,1,0,2:T(8,128)(2,1)} copy(bf16[2,1024,4,512]{1,3,0,2:T(8,128)(2,1)} %bitcast.124) | data formatting | bytes 16777216 | tf_op jit(solution)/shard_map/acnf,ang->cfg/dot_general | solution.py:135
  603.6 11.5 %copy.67 = bf16[2,1024,4,512]{3,1,0,2:T(8,128)(2,1)} copy(bf16[2,1024,4,512]{1,3,0,2:T(8,128)(2,1)} %bitcast.126) | data formatting | bytes 16777216 | tf_op jit(solution)/shard_map/acnf,ang->cfg/dot_general | solution.py:138
  615.1 128.2 %all-reduce.3.cloned.1.call-done = (bf16[4,512,1024]{2,1,0:T(8,128)(2,1)}, bf16[4,512,1024]{2,1,0:T(8,128)(2,1)}) async-done(((bf16[4,512,1024]{2,1,0:T(8,128)(2,1)}, bf16[4,512,1024]{2,1,0:T(8,128)(2,1)}), (bf16[4,512,1024]{2,1,0:T(8,128)(2,1)}, bf16[4,512,1024]{2,1,0:T(8,128)(2,1)})) %all-reduce.3.cloned.1.call-update) | async-done | bytes 8388624 | tf_op jit(solution)/shard_map/psum | solution.py:13
  743.3 14.6 %bitcast_multiply_fusion.1 = f32[2048,1024]{1,0:T(8,128)} fusion(bf16[2048,4,512]{2,0,1:T(8,128)(2,1)} %bitcast.128, bf16[4,512,1024]{2,1,0:T(8,128)(2,1)} %get-tuple-element.383), kind=kOutput, calls=%fused_computation.43 | convolution fusion | flops 8592031744 | bytes 20971520 | tf_op jit(solution)/shard_map/acnf,ang->cfg/dot_general | solution.py:135
  757.9 11.0 %bitcast_multiply_fusion = f32[2048,1024]{1,0:T(8,128)} fusion(bf16[2048,4,512]{2,0,1:T(8,128)(2,1)S(1)} %bitcast.127, bf16[4,512,1024]{2,1,0:T(8,128)(2,1)S(1)} %copy-done.4), kind=kOutput, calls=%fused_computation.42 | convolution fusion | flops 8592031744 | bytes 20971520 | tf_op jit(solution)/shard_map/acnf,ang->cfg/dot_general | solution.py:138
  (76 shorter events, 1.4 us)
Async XLA Ops:
  7.2 86.1 %copy-start = (bf16[512,1024]{1,0:T(8,128)(2,1)S(1)}, bf16[512,1024]{1,0:T(8,128)(2,1)}, u32[]{:S(2)}) copy-start(bf16[512,1024]{1,0:T(8,128)(2,1)} %param.9) | copy-start | bytes 3145732
  7.2 86.1 %copy-start.3 = (s32[6]{0:T(128)S(1)}, s32[6]{0:T(128)}, u32[]{:S(2)}) copy-start(s32[6]{0:T(128)} %param.13) | copy-start | bytes 76
  7.2 86.0 %all-gather.9.cloned.1.call-start = ((), (), s32[]{:S(2)}) async-start(), calls=%async_computation.1 | async-start | bytes 5242880 | tf_op jit(solution)/shard_map/all_gather | solution.py:39
  9.6 165.0 %all-gather.7.cloned.1.call-start = ((), (), s32[]{:S(2)}) async-start(), calls=%async_computation | async-start | bytes 5242880 | tf_op jit(solution)/shard_map/all_gather | solution.py:40
  12.0 243.5 %all-gather.15.cloned.1.call-start = ((), (), s32[]{:S(2)}) async-start(), calls=%async_computation.4 | async-start | bytes 5242880 | tf_op jit(solution)/shard_map/all_gather | solution.py:105
  12.7 324.2 %all-gather.13.cloned.1.call-start = ((), (), s32[]{:S(2)}) async-start(), calls=%async_computation.3 | async-start | bytes 5242880 | tf_op jit(solution)/shard_map/all_gather | solution.py:104
  15.0 447.3 %all-gather.11.cloned.1.call-start = ((), (), s32[]{:S(2)}) async-start(), calls=%async_computation.2 | async-start | bytes 9437184 | tf_op jit(solution)/shard_map/all_gather | solution.py:122
  208.8 128.1 %copy-start.2 = (bf16[512,1024]{1,0:T(8,128)(2,1)S(1)}, bf16[512,1024]{1,0:T(8,128)(2,1)}, u32[]{:S(2)}) copy-start(bf16[512,1024]{1,0:T(8,128)(2,1)} %param.10) | copy-start | bytes 3145732
  212.0 375.6 %all-gather.17.cloned.1.call-start = ((), (), s32[]{:S(2)}) async-start(), calls=%async_computation.5 | async-start | bytes 9437184 | tf_op jit(solution)/shard_map/all_gather | solution.py:123
  352.7 390.6 %all-reduce.3.cloned.1.call-start = ((), (), s32[]{:S(2)}) async-start(), calls=%async_computation.6 | async-start | bytes 16777216 | tf_op jit(solution)/shard_map/psum | solution.py:13
  743.3 14.6 %copy-start.1 = (bf16[2,1024,4,512]{3,1,0,2:T(8,128)(2,1)S(1)}, bf16[2,1024,4,512]{3,1,0,2:T(8,128)(2,1)}, u32[]{:S(2)}) copy-start(bf16[2,1024,4,512]{3,1,0,2:T(8,128)(2,1)} %copy.67) | copy-start | bytes 25165828
  743.3 14.6 %copy-start.4 = (bf16[4,512,1024]{2,1,0:T(8,128)(2,1)S(1)}, bf16[4,512,1024]{2,1,0:T(8,128)(2,1)}, u32[]{:S(2)}) copy-start(bf16[4,512,1024]{2,1,0:T(8,128)(2,1)} %get-tuple-element.384) | copy-start | bytes 12582916
Sparse Core Ops, SparseCore 0:
  9.7 83.4 all-gather.8
  95.4 79.2 all-gather.6
  176.2 79.2 all-gather.14
  256.9 79.9 all-gather.12
  339.5 122.8 all-gather.10
  464.9 122.6 all-gather.16
  592.2 151.0 all-reduce.2
where the time goes:
time: 777 us; the launch traced here: 776 us
  waiting for transfers between devices  594 us (76%)
  matrix products  67.8 us (9%)
  local copies, waits for them, and re-layouts  56 us (7%)
  other arithmetic  22.4 us (3%)
  blocking collectives  15.2 us (2%)
  between operations  14.2 us (2%)
    psum x1, waiting for transfers between devices, spread(): return lax.psum(kept, axis)  128 us
    all_gather x1, waiting for transfers between devices, on_device(): lax.all_gather(value_grads[None], ('tokens', 'cols'), axis=0, tiled=True)  121 us
    all_gather x1, waiting for transfers between devices, on_device(): lax.all_gather(attended[None], ('tokens', 'cols'), axis=0, tiled=True)  109 us
    all_gather x1, waiting for transfers between devices, on_device(): lax.all_gather(key_in, 'tokens', axis=0, tiled=True)  78.1 us
    all_gather x1, waiting for transfers between devices, on_device(): query_rows = lax.all_gather(query_in, 'tokens', axis=0, tiled=True)  59.8 us
    all_gather x1, waiting for transfers between devices, on_device(): lax.all_gather(value_in, 'tokens', axis=0, tiled=True)  54.3 us
    all_gather x1, waiting for transfers between devices, on_device(): grad_rows = lax.all_gather(out_grads, 'tokens', axis=0, tiled=True)  42.4 us
    dot_general x4, matrix products, update(): jnp.einsum('hqk,khd->qhd', weights, value_rows, preferred_element_type=jn...  20.8 us
  transfers between devices with their start and end apart: 7, of which 7 were waited for; matrix products, arithmetic and copies ran while one was open for 15% of the time, Pallas kernels for 0%

commit v1 on v0

--- a/solution.py
+++ b/solution.py
@@ -10,7 +10,7 @@
 
 def spread(value, axis, source):
     kept = jnp.where(lax.axis_index(axis) == source, value, 0).astype(value.dtype)
-    return lax.psum(kept, axis)
+    return jnp.sum(lax.all_gather(kept, axis), axis=0)
 
 
 def document_ids(positions, doc_starts):

time: 777 us -> 845 us (1.088)
  other arithmetic: 22.4 us -> 56.6 us
  waiting for transfers between devices: 594 us -> 615 us
  matrix products: 67.8 us -> 80.2 us
    all_gather x0 -> x2, waiting for transfers between devices: none -> 173 us  [spread(): return jnp.sum(lax.all_gather(kept, axis), axis=0)]
    psum x1 -> x0, waiting for transfers between devices: 128 us -> none  [spread(): return lax.psum(kept, axis)]
    all_gather x1, waiting for transfers between devices: 54.3 us -> 30.1 us  [on_device(): lax.all_gather(value_in, 'tokens', axis=0, tiled=True)]
    unnamed x3 -> x6, other arithmetic: 0.01 us -> 23.9 us
    dot_general x4, matrix products: 6.96 us -> 20.6 us  [pair_scores(): jnp.einsum('qhd,khd->hqk', query_heads, key_heads, preferred_element_type...]
    reduce_sum x4, other arithmetic: 8.14 us -> 18.3 us  [update(): jnp.sum(jnp.where(allowed, jnp.exp(masked - new_peak[:, :, None]), 0.0),...]
  transfers between devices with their start and end apart: 7 -> 8, of which waited for: 7 -> 8; matrix products, arithmetic and copies ran while one was open for 15% -> 18% of each run, Pallas kernels for 0% -> 0%
where the time goes in v1:
time: 845 us; the launch traced here: 843 us
  waiting for transfers between devices  615 us (73%)
  matrix products  80.2 us (9%)
  other arithmetic  56.6 us (7%)
  local copies, waits for them, and re-layouts  56.4 us (7%)
  blocking collectives  15.2 us (2%)
  between operations  14.3 us (2%)
    all_gather x2, waiting for transfers between devices, spread(): return jnp.sum(lax.all_gather(kept, axis), axis=0)  173 us
    all_gather x1, waiting for transfers between devices, on_device(): lax.all_gather(value_grads[None], ('tokens', 'cols'), axis=0, tiled=True)  120 us
    all_gather x1, waiting for transfers between devices, on_device(): lax.all_gather(attended[None], ('tokens', 'cols'), axis=0, tiled=True)  110 us
    all_gather x1, waiting for transfers between devices, on_device(): lax.all_gather(key_in, 'tokens', axis=0, tiled=True)  78.5 us
    all_gather x1, waiting for transfers between devices, on_device(): query_rows = lax.all_gather(query_in, 'tokens', axis=0, tiled=True)  59.8 us
    all_gather x1, waiting for transfers between devices, on_device(): grad_rows = lax.all_gather(out_grads, 'tokens', axis=0, tiled=True)  42.4 us
    all_gather x1, waiting for transfers between devices, on_device(): lax.all_gather(value_in, 'tokens', axis=0, tiled=True)  30.1 us
    unnamed x6, other arithmetic  23.9 us
  transfers between devices with their start and end apart: 8, of which 8 were waited for; matrix products, arithmetic and copies ran while one was open for 18% of the time, Pallas kernels for 0%

profile of v1, /device:TPU:0, one launch (start us, length us, event | category | flops | bytes accessed | tf_op | source)
XLA Modules:
  0.0 843.5 jit_solution(14831967319808678650)
XLA Ops:
  7.2 2.4 copy.56
  9.7 2.3 copy.55
  12.0 0.7 all-gather.19.cloned.1.call-update
  12.7 2.3 copy.61
  15.1 78.5 %all-gather.13.cloned.1.call-done = bf16[2048,1024]{0,1:T(8,128)(2,1)} async-done(((bf16[512,1024]{0,1:T(8,128)(2,1)}), bf16[2048,1024]{0,1:T(8,128)(2,1)}) %all-gather.13.cloned.1.call-update) | async-done | bytes 4194320 | tf_op jit(solution)/shard_map/all_gather | solution.py:39
  93.6 50.7 %while.30 = (s32[]{:T(128)}, f32[8,512]{1,0:T(8,128)S(1)}, f32[8,512]{1,0:T(8,128)S(1)}, s32[6]{0:T(128)S(1)}, s32[4]{0:T(128)S(1)}, /*index=5*/bf16[2048,1024]{...) while((s32[]{:T(128)}, f32[8,512]{1,0:T(8,128)S(1)}, ...), condition=%wide.region_5.6_spmd.clone, body=%wide.region_0.5_spmd.clone.sunk | while | flops 553950208 | bytes 21995740 | solution.py:75
  93.6 0.6 dynamic_slice.60
  95.0 0.2 broadcast_compare_fusion.5
  95.2 1.3 constant_dynamic-slice_fusion.5
  96.5 5.2 fusion.57
  101.7 4.9 select_reduce_fusion.2
  106.6 0.6 dynamic_slice.60
  108.0 0.2 broadcast_compare_fusion.5
  108.2 1.3 constant_dynamic-slice_fusion.5
  109.5 5.1 fusion.57
  114.7 4.5 select_reduce_fusion.2
  119.2 0.6 dynamic_slice.60
  120.6 0.2 broadcast_compare_fusion.5
  120.8 1.3 constant_dynamic-slice_fusion.5
  122.1 5.1 fusion.57
  127.3 4.5 select_reduce_fusion.2
  131.8 0.6 dynamic_slice.60
  133.2 0.2 broadcast_compare_fusion.5
  133.4 1.3 constant_dynamic-slice_fusion.5
  134.7 5.1 fusion.57
  139.8 4.5 select_reduce_fusion.2
  144.4 30.1 %all-gather.11.cloned.1.call-done = bf16[2048,1024]{0,1:T(8,128)(2,1)} async-done(((bf16[512,1024]{0,1:T(8,128)(2,1)}), bf16[2048,1024]{0,1:T(8,128)(2,1)}) %all-gather.11.cloned.1.call-update) | async-done | bytes 4194320 | tf_op jit(solution)/shard_map/all_gather | solution.py:40
  174.5 34.2 %while.31 = (s32[]{:T(128)}, f32[512,8,128]{0,2,1:T(8,128)}, s32[4]{0:T(128)S(1)}, bf16[2048,1024]{0,1:T(8,128)(2,1)}, s32[6]{0:T(128)S(1)}, /*index=5*/bf16[204...) while((s32[]{:T(128)}, f32[512,8,128]{0,2,1:T(8,128)}, ...), condition=%wide.region_9.10_spmd.clone, body=%wide.region_6.9_spmd.clone.sunk | while | flops 1083460608 | bytes 12099813 | solution.py:101
  174.5 0.6 dynamic_slice.62
  175.8 0.2 broadcast_compare_fusion.6
  176.1 1.7 constant_dynamic-slice_fusion.6
  177.8 4.0 bitcast_add_fusion.2
  181.8 0.6 dynamic_slice.62
  183.1 0.2 broadcast_compare_fusion.6
  183.4 1.9 constant_dynamic-slice_fusion.6
  185.3 5.6 bitcast_add_fusion.2
  190.9 0.6 dynamic_slice.62
  192.5 1.7 constant_dynamic-slice_fusion.6
  194.2 5.6 bitcast_add_fusion.2
  199.8 0.6 dynamic_slice.62
  201.4 1.7 constant_dynamic-slice_fusion.6
  203.1 5.6 bitcast_add_fusion.2
  208.7 1.8 convert_element_type.80
  210.5 1.3 copy.75
  212.1 0.8 broadcast_compare_fusion.2
  212.9 42.4 %all-gather.19.cloned.1.call-done = bf16[2048,1024]{1,0:T(8,128)(2,1)} async-done(((bf16[512,1024]{1,0:T(8,128)(2,1)}), bf16[2048,1024]{1,0:T(8,128)(2,1)}) %all-gather.19.cloned.1.call-update) | async-done | bytes 4194320 | tf_op jit(solution)/shard_map/all_gather | solution.py:105
  255.3 6.4 copy.64
  261.7 15.2 %all_gather.34 = f32[2048,8]{0,1:T(8,128)S(1)} all-gather(f32[512,8]{0,1:T(8,128)S(1)} %bitcast.130), channel_id=1, replica_groups=mesh['heads'=4,'tokens'=4,'cols'=2] {'tokens'}, dimensions={0}, use_global_device_ids=true | all-gather | bytes 81920 | tf_op jit(solution)/shard_map/all_gather | solution.py:103
  277.0 59.8 %all-gather.17.cloned.1.call-done = bf16[2048,1024]{0,1:T(8,128)(2,1)} async-done(((bf16[512,1024]{0,1:T(8,128)(2,1)}), bf16[2048,1024]{0,1:T(8,128)(2,1)}) %all-gather.17.cloned.1.call-update) | async-done | bytes 4194320 | tf_op jit(solution)/shard_map/all_gather | solution.py:104
  336.8 14.4 %fusion.27 = bf16[8,512,128]{1,2,0:T(8,128)(2,1)S(1)} fusion(bf16[2048,8,128]{0,2,1:T(8,128)(2,1)} %bitcast.128, bf16[2048,8,128]{0,2,1:T(8,128)(2,1)} %bitcast.132, f32[8,2048]{1,0:T(8,128)S(1)} %bitcast.131, pred[2048,512]{1,0:T(8,128)(4,1)S(1)} %broadcast_compare_fusion.2, bf16[512,1024]{1,0:T(8,128)(2,1)S(1)} %copy-done.2), kind=kOutput, calls=%fused_computation.50 | convolution fusion | flops 4329046016 | bytes 11599872 | tf_op jit(solution)/shard_map/hqk,qhd->khd/dot_general | solution.py:115
  351.2 1.3 copy.65
  352.6 109.7 %all-gather.15.cloned.1.call-done = bf16[8,512,1024]{2,1,0:T(8,128)(2,1)} async-done(((bf16[1,512,1024]{2,1,0:T(8,128)(2,1)}), bf16[8,512,1024]{2,1,0:T(8,128)(2,1)}) %all-gather.15.cloned.1.call-update) | async-done | bytes 8388624 | tf_op jit(solution)/shard_map/all_gather | solution.py:122
  462.2 4.5 dynamic-slice_select_fusion.1
  466.7 0.3 all-gather.25.cloned.1.call-start
  467.0 120.5 %all-gather.21.cloned.1.call-done = bf16[8,512,1024]{2,1,0:T(8,128)(2,1)} async-done(((bf16[1,512,1024]{2,1,0:T(8,128)(2,1)}), bf16[8,512,1024]{2,1,0:T(8,128)(2,1)}) %all-gather.21.cloned.1.call-update) | async-done | bytes 8388624 | tf_op jit(solution)/shard_map/all_gather | solution.py:123
  587.5 4.5 dynamic-slice_select_fusion
  592.0 12.0 %copy.58 = bf16[2,1024,4,512]{3,1,0,2:T(8,128)(2,1)} copy(bf16[2,1024,4,512]{1,3,0,2:T(8,128)(2,1)} %bitcast.118) | data formatting | bytes 16777216 | tf_op jit(solution)/shard_map/acnf,ang->cfg/dot_general | solution.py:135
  604.0 11.5 %copy.66 = bf16[2,1024,4,512]{3,1,0,2:T(8,128)(2,1)} copy(bf16[2,1024,4,512]{1,3,0,2:T(8,128)(2,1)} %bitcast.120) | data formatting | bytes 16777216 | tf_op jit(solution)/shard_map/acnf,ang->cfg/dot_general | solution.py:138
  615.6 78.2 %all-gather.23.cloned.1.call-done = bf16[16,1,512,1024]{3,2,1,0:T(8,128)(2,1)} async-done(((bf16[4,1,512,1024]{3,2,1,0:T(8,128)(2,1)}), bf16[16,1,512,1024]{3,2,1,0:T(8,128)(2,1)}) %all-gather.23.cloned.1.call-update) | async-done | bytes 16777232 | tf_op jit(solution)/shard_map/all_gather | solution.py:13
  693.7 12.8 %bitcast_reduce_fusion.1 = bf16[4,512,1024]{2,1,0:T(8,128)(2,1)} fusion(bf16[4,4,512,1024]{3,2,1,0:T(8,128)(2,1)} %bitcast.121), kind=kLoop, calls=%fused_computation.43 | loop fusion | flops 6291456 | bytes 20971520
  706.5 94.7 %all-gather.25.cloned.1.call-done = bf16[16,1,512,1024]{3,2,1,0:T(8,128)(2,1)} async-done(((bf16[4,1,512,1024]{3,2,1,0:T(8,128)(2,1)}), bf16[16,1,512,1024]{3,2,1,0:T(8,128)(2,1)}) %all-gather.25.cloned.1.call-update) | async-done | bytes 16777232 | tf_op jit(solution)/shard_map/all_gather | solution.py:13
  801.2 11.0 %bitcast_reduce_fusion = bf16[4,512,1024]{2,1,0:T(8,128)(2,1)S(1)} fusion(bf16[4,4,512,1024]{3,2,1,0:T(8,128)(2,1)} %bitcast.122), kind=kLoop, calls=%fused_computation.42 | loop fusion | flops 6291456 | bytes 20971520
  812.3 13.4 %bitcast_multiply_fusion.1 = f32[2048,1024]{1,0:T(8,128)} fusion(bf16[2048,4,512]{2,0,1:T(8,128)(2,1)} %bitcast.126, bf16[4,512,1024]{2,1,0:T(8,128)(2,1)S(1)} %copy-done.1), kind=kOutput, calls=%fused_computation.45 | convolution fusion | flops 8592031744 | bytes 20971520 | tf_op jit(solution)/shard_map/acnf,ang->cfg/dot_general | solution.py:135
  825.6 11.0 %bitcast_multiply_fusion = f32[2048,1024]{1,0:T(8,128)} fusion(bf16[2048,4,512]{2,0,1:T(8,128)(2,1)S(1)} %bitcast.125, bf16[4,512,1024]{2,1,0:T(8,128)(2,1)S(1)} %bitcast_reduce_fusion), kind=kOutput, calls=%fused_computation.44 | convolution fusion | flops 8592031744 | bytes 20971520 | tf_op jit(solution)/shard_map/acnf,ang->cfg/dot_general | solution.py:138
  (84 shorter events, 2.0 us)
Async XLA Ops:
  7.2 86.5 %copy-start = (bf16[512,1024]{1,0:T(8,128)(2,1)S(1)}, bf16[512,1024]{1,0:T(8,128)(2,1)}, u32[]{:S(2)}) copy-start(bf16[512,1024]{1,0:T(8,128)(2,1)} %param.9) | copy-start | bytes 3145732
  7.2 86.5 %copy-start.3 = (s32[6]{0:T(128)S(1)}, s32[6]{0:T(128)}, u32[]{:S(2)}) copy-start(s32[6]{0:T(128)} %param.13) | copy-start | bytes 76
  7.2 86.4 %all-gather.13.cloned.1.call-start = ((), (), s32[]{:S(2)}) async-start(), calls=%async_computation.1 | async-start | bytes 5242880 | tf_op jit(solution)/shard_map/all_gather | solution.py:39
  9.6 164.8 %all-gather.11.cloned.1.call-start = ((), (), s32[]{:S(2)}) async-start(), calls=%async_computation | async-start | bytes 5242880 | tf_op jit(solution)/shard_map/all_gather | solution.py:40
  12.0 243.3 %all-gather.19.cloned.1.call-start = ((), (), s32[]{:S(2)}) async-start(), calls=%async_computation.4 | async-start | bytes 5242880 | tf_op jit(solution)/shard_map/all_gather | solution.py:105
  12.7 324.1 %all-gather.17.cloned.1.call-start = ((), (), s32[]{:S(2)}) async-start(), calls=%async_computation.3 | async-start | bytes 5242880 | tf_op jit(solution)/shard_map/all_gather | solution.py:104
  15.0 447.2 %all-gather.15.cloned.1.call-start = ((), (), s32[]{:S(2)}) async-start(), calls=%async_computation.2 | async-start | bytes 9437184 | tf_op jit(solution)/shard_map/all_gather | solution.py:122
  208.7 128.1 %copy-start.2 = (bf16[512,1024]{1,0:T(8,128)(2,1)S(1)}, bf16[512,1024]{1,0:T(8,128)(2,1)}, u32[]{:S(2)}) copy-start(bf16[512,1024]{1,0:T(8,128)(2,1)} %param.10) | copy-start | bytes 3145732
  211.9 375.6 %all-gather.21.cloned.1.call-start = ((), (), s32[]{:S(2)}) async-start(), calls=%async_computation.5 | async-start | bytes 9437184 | tf_op jit(solution)/shard_map/all_gather | solution.py:123
  352.5 341.2 %all-gather.23.cloned.1.call-start = ((), (), s32[]{:S(2)}) async-start(), calls=%async_computation.6 | async-start | bytes 20971520 | tf_op jit(solution)/shard_map/all_gather | solution.py:13
  466.7 334.5 %all-gather.25.cloned.1.call-start = ((), (), s32[]{:S(2)}) async-start(), calls=%async_computation.7 | async-start | bytes 20971520 | tf_op jit(solution)/shard_map/all_gather | solution.py:13
  801.2 11.0 %copy-start.1 = (bf16[4,512,1024]{2,1,0:T(8,128)(2,1)S(1)}, bf16[4,512,1024]{2,1,0:T(8,128)(2,1)}, u32[]{:S(2)}) copy-start(bf16[4,512,1024]{2,1,0:T(8,128)(2,1)} %bitcast_reduce_fusion.1) | copy-start | bytes 12582916
  801.2 24.4 %slice-start = ((s8[8388608]{0:T(1024)(128)(4,1)}), s8[4194304]{0:T(1024)(128)(4,1)S(1)}, s32[]{:S(2)}) async-start(s8[8388608]{0:T(1024)(128)(4,1)} %bitcast.123), calls=%async_computation.8 | async-start | bytes 8388608
  812.2 13.4 %slice-start.1 = ((s8[8388608]{0:T(1024)(128)(4,1)}), s8[4194304]{0:T(1024)(128)(4,1)S(1)}, s32[]{:S(2)}) async-start(s8[8388608]{0:T(1024)(128)(4,1)} %bitcast.123), calls=%async_computation.9 | async-start | bytes 8388608
Sparse Core Ops, SparseCore 0:
  10.1 83.4 all-gather.12
  95.2 79.2 all-gather.10
  176.0 79.2 all-gather.18
  256.7 79.9 all-gather.16
  339.3 122.8 all-gather.14
  464.8 122.6 all-gather.20
  589.6 104.0 all-gather.22
  695.3 105.8 all-gather.24
